TPU v7x, 128 devices: a whole 4x4x4 slice. The times are simulated.
128 devices in a mesh: row: 16 (over y, x), col: 8 (over z, core).
Axes of the slice: x: 4, y: 4, z: 4, core: 2. Of those that a mesh axis runs over, the one named last changes fastest.
Arguments:
- features: bfloat16 [65536, 512], P('col', 'row'), may hold values from -6 to 6
- weight_t: bfloat16 [512, 512], P(None, 'row'), may hold values from -0.25 to 0.25
- tiles: bfloat16 [32768, 128, 128], P(('row', 'col')), may hold values from -0.109375 to 0.109375
- coords: int32 [2, 32768], P(None, ('row', 'col')), may hold values from 0 to 63, as said below
- counts: int32 [128], P(('row', 'col')), may hold values from 32 to 256, as said below
Outputs:
- output: bfloat16 [65536, 512], P('row', 'col')
Inputs may be any that keep to these rules, and one draw needn't show every extreme that they name: coords[0] of a slot lies in 0 to 31 and coords[1] in 0 to 63; the live slots of one grid cell name distinct tiles. `counts`: some grid cell has all 256 slots live in every draw.
All inputs are finite; a program needn't handle non-finite values.
Results may differ from a plain program's by a relative error of at most 0.0095.
Values may be sent and summed in bfloat16 or wider, within the bound.
A program may use at most 128 MiB of HBM per device.

v0:
```python
import jax
import jax.numpy as jnp
from jax import lax
from jax.sharding import PartitionSpec as P

TROW = 32


def rows_first(arrays, axis, dims):
    turned = [jnp.moveaxis(a, dim, 0) for a, dim in zip(arrays, dims)]
    widths = [t[0].size for t in turned]
    both = jnp.concatenate([t.reshape(-1, w) for t, w in zip(turned, widths)], axis=1)
    result = lax.all_gather(both, axis, axis=0, tiled=True)
    tiles = jnp.split(result, [sum(widths[:k]) for k in range(1, len(widths))], axis=1)
    return tuple(
        (
            jnp.moveaxis(b.reshape(-1, *t.shape[1:]), 0, dim)
            for b, t, dim in zip(tiles, turned, dims)
        )
    )


def tile_apply(tiles, rows, cols, count, source):
    maxt = tiles.shape[0]
    tile = tiles.shape[1]
    width = source.shape[2]
    tcol_here = source.shape[0]
    group = min(32, maxt)
    offsets = jnp.arange(group, dtype=jnp.int32)
    col_lanes = jnp.arange(tcol_here, dtype=jnp.int32)
    row_lanes = jnp.arange(TROW, dtype=jnp.int32)

    def step(index, total):
        start = (index * group).astype(jnp.int32)
        block = lax.dynamic_slice_in_dim(tiles, start, group, 0)
        block_rows = lax.dynamic_slice_in_dim(rows, start, group, 0)
        block_cols = lax.dynamic_slice_in_dim(cols, start, group, 0)
        live = start + offsets < count
        pick_cols = (block_cols[:, None] == col_lanes[None, :]).astype(jnp.bfloat16)
        inputs = jnp.einsum(
            "gc,cjw->gjw", pick_cols, source, preferred_element_type=jnp.float32
        ).astype(jnp.bfloat16)
        prod = jnp.einsum("gij,gjw->giw", block, inputs, preferred_element_type=jnp.float32)
        place_rows = ((block_rows[:, None] == row_lanes[None, :]) & live[:, None]).astype(
            jnp.float32
        )
        added = jnp.einsum("gt,giw->tiw", place_rows, prod)
        return total + added

    turns = maxt // group
    total = lax.fori_loop(0, turns, step, jnp.zeros((TROW, tile, width), jnp.float32))
    return total.reshape(TROW * tile, width)


def body(features, weight_t, tiles, coords, counts):
    rows = coords[0]
    cols = coords[1]
    count = counts[0]
    tile = tiles.shape[1]
    tcol_here = features.shape[0] // tile
    panel, weight_full = rows_first((features, weight_t), "row", (1, 1))
    spread = tile_apply(tiles, rows, cols, count, panel.reshape(tcol_here, tile, panel.shape[1]))
    partial_value = lax.dot_general(
        spread, weight_full.astype(jnp.float32), (((1,), (1,)), ((), ()))
    )
    summed = lax.psum_scatter(partial_value, "col", scatter_dimension=1, tiled=True)
    return summed.astype(jnp.bfloat16)


def solution(mesh):
    placed = (
        P("col", "row"),
        P(None, "row"),
        P(("row", "col"), None, None),
        P(None, ("row", "col")),
        P(("row", "col")),
    )
    return jax.shard_map(
        body, mesh=mesh, in_specs=placed, out_specs=P("row", "col"), check_vma=False
    )
```

profile of v0, /device:TPU:1, one launch (start us, length us, event | category | flops | bytes accessed | tf_op | source)
XLA Modules:
  0.0 411.9 jit_solution(2811243389404813763)
XLA Ops:
  9.3 76.2 %all-gather.2.cloned.1.call-done = bf16[512,8704]{1,0:T(8,128)(2,1)} async-done(((bf16[32,8704]{1,0:T(8,128)(2,1)}), bf16[512,8704]{1,0:T(8,128)(2,1)}) %all-gather.2.cloned.1.call-update) | async-done | bytes 8912912 | tf_op jit(solution)/shard_map/all_gather | solution.py:13
  85.6 7.6 %slice_bitcast_fusion = bf16[8192,512]{0,1:T(8,128)(2,1)} fusion(bf16[512,8704]{1,0:T(8,128)(2,1)} %all-gather.2.cloned.1.call-done), kind=kLoop, calls=%fused_computation.21 | loop fusion | bytes 16777216 | tf_op jit(solution)/shard_map/transpose | solution.py:17
  93.2 11.9 %copy.7 = bf16[8192,512]{1,0:T(8,128)(2,1)} copy(bf16[8192,512]{0,1:T(8,128)(2,1)} %slice_bitcast_fusion) | data formatting | bytes 16777216 | tf_op jit(solution)/shard_map/transpose | solution.py:17
  105.1 231.3 %while.16 = (s32[]{:T(128)}, f32[32,128,512]{2,0,1:T(8,128)}, s32[256]{0:T(256)S(1)}, s32[]{:T(128)}, bf16[256,128,128]{2,1,0:T(8,128)(2,1)}, /*index=5*/s32[256...) while((s32[]{:T(128)}, f32[32,128,512]{2,0,1:T(8,128)}, ...), condition=%wide.region_1.0_spmd.clone.clone, body=%wide.region_0.0_spmd.clone.clone.sunk | while | flops 943722560 | bytes 101712968 | solution.py:51
  105.9 13.5 %fusion.39 = bf16[32,128,512]{2,0,1:T(8,128)(2,1)S(1)} fusion(bf16[64,128,512]{2,1,0:T(8,128)(2,1)} %get-tuple-element.326, s32[32]{0:T(128)S(1)} %dynamic_slice.36), kind=kOutput, calls=%fused_computation.5.clone.1 | convolution fusion | flops 268437504 | bytes 12583040 | tf_op jit(solution)/shard_map/while/body/eval_jaxpr/gc,cjw->gjw/dot_general | solution.py:40
  119.5 6.3 %fusion.40 = bf16[32,128,512]{2,1,0:T(8,128)(2,1)S(1)} fusion(bf16[32,128,512]{2,0,1:T(8,128)(2,1)S(1)} %fusion.39, bf16[256,128,128]{2,1,0:T(8,128)(2,1)} %get-tuple-element.324, s32[]{:T(128)S(6)} %select_n.13), kind=kOutput, calls=%fused_computation.8.clone.1 | convolution fusion | flops 536870912 | bytes 9437188 | tf_op jit(solution)/shard_map/while/body/eval_jaxpr/gij,gjw->giw/dot_general | solution.py:43
  134.8 13.5 %fusion.39 = bf16[32,128,512]{2,0,1:T(8,128)(2,1)S(1)} fusion(bf16[64,128,512]{2,1,0:T(8,128)(2,1)} %get-tuple-element.326, s32[32]{0:T(128)S(1)} %dynamic_slice.36), kind=kOutput, calls=%fused_computation.5.clone.1 | convolution fusion | flops 268437504 | bytes 12583040 | tf_op jit(solution)/shard_map/while/body/eval_jaxpr/gc,cjw->gjw/dot_general | solution.py:40
  148.4 6.3 %fusion.40 = bf16[32,128,512]{2,1,0:T(8,128)(2,1)S(1)} fusion(bf16[32,128,512]{2,0,1:T(8,128)(2,1)S(1)} %fusion.39, bf16[256,128,128]{2,1,0:T(8,128)(2,1)} %get-tuple-element.324, s32[]{:T(128)S(6)} %select_n.13), kind=kOutput, calls=%fused_computation.8.clone.1 | convolution fusion | flops 536870912 | bytes 9437188 | tf_op jit(solution)/shard_map/while/body/eval_jaxpr/gij,gjw->giw/dot_general | solution.py:43
  154.7 4.9 %select_add_fusion.2 = f32[32,128,512]{2,0,1:T(8,128)S(1)} fusion(f32[32,128,512]{2,0,1:T(8,128)S(1)} %bitcast.22, pred[]{:T(512)S(6)} %compare.3, bf16[32,128,512]{2,1,0:T(8,128)(2,1)S(1)} %fusion.40, s32[32]{0:T(128)S(1)} %dynamic_slice.37, pred[32]{0:T(512)(128)(4,1)S(1)} %fusion.41), kind=kOutput, calls=%fused_computation.7.clone.1 | convolution fusion | flops 138414080 | bytes 20971680 | tf_op jit(solution)/shard_map/while/body/eval_jaxpr/gt,giw->tiw/dot_general | solution.py:47
  163.7 13.5 %fusion.39 = bf16[32,128,512]{2,0,1:T(8,128)(2,1)S(1)} fusion(bf16[64,128,512]{2,1,0:T(8,128)(2,1)} %get-tuple-element.326, s32[32]{0:T(128)S(1)} %dynamic_slice.36), kind=kOutput, calls=%fused_computation.5.clone.1 | convolution fusion | flops 268437504 | bytes 12583040 | tf_op jit(solution)/shard_map/while/body/eval_jaxpr/gc,cjw->gjw/dot_general | solution.py:40
  177.3 6.3 %fusion.40 = bf16[32,128,512]{2,1,0:T(8,128)(2,1)S(1)} fusion(bf16[32,128,512]{2,0,1:T(8,128)(2,1)S(1)} %fusion.39, bf16[256,128,128]{2,1,0:T(8,128)(2,1)} %get-tuple-element.324, s32[]{:T(128)S(6)} %select_n.13), kind=kOutput, calls=%fused_computation.8.clone.1 | convolution fusion | flops 536870912 | bytes 9437188 | tf_op jit(solution)/shard_map/while/body/eval_jaxpr/gij,gjw->giw/dot_general | solution.py:43
  192.7 13.5 %fusion.39 = bf16[32,128,512]{2,0,1:T(8,128)(2,1)S(1)} fusion(bf16[64,128,512]{2,1,0:T(8,128)(2,1)} %get-tuple-element.326, s32[32]{0:T(128)S(1)} %dynamic_slice.36), kind=kOutput, calls=%fused_computation.5.clone.1 | convolution fusion | flops 268437504 | bytes 12583040 | tf_op jit(solution)/shard_map/while/body/eval_jaxpr/gc,cjw->gjw/dot_general | solution.py:40
  206.2 6.3 %fusion.40 = bf16[32,128,512]{2,1,0:T(8,128)(2,1)S(1)} fusion(bf16[32,128,512]{2,0,1:T(8,128)(2,1)S(1)} %fusion.39, bf16[256,128,128]{2,1,0:T(8,128)(2,1)} %get-tuple-element.324, s32[]{:T(128)S(6)} %select_n.13), kind=kOutput, calls=%fused_computation.8.clone.1 | convolution fusion | flops 536870912 | bytes 9437188 | tf_op jit(solution)/shard_map/while/body/eval_jaxpr/gij,gjw->giw/dot_general | solution.py:43
  221.6 13.5 %fusion.39 = bf16[32,128,512]{2,0,1:T(8,128)(2,1)S(1)} fusion(bf16[64,128,512]{2,1,0:T(8,128)(2,1)} %get-tuple-element.326, s32[32]{0:T(128)S(1)} %dynamic_slice.36), kind=kOutput, calls=%fused_computation.5.clone.1 | convolution fusion | flops 268437504 | bytes 12583040 | tf_op jit(solution)/shard_map/while/body/eval_jaxpr/gc,cjw->gjw/dot_general | solution.py:40
  235.1 6.3 %fusion.40 = bf16[32,128,512]{2,1,0:T(8,128)(2,1)S(1)} fusion(bf16[32,128,512]{2,0,1:T(8,128)(2,1)S(1)} %fusion.39, bf16[256,128,128]{2,1,0:T(8,128)(2,1)} %get-tuple-element.324, s32[]{:T(128)S(6)} %select_n.13), kind=kOutput, calls=%fused_computation.8.clone.1 | convolution fusion | flops 536870912 | bytes 9437188 | tf_op jit(solution)/shard_map/while/body/eval_jaxpr/gij,gjw->giw/dot_general | solution.py:43
  250.5 13.5 %fusion.39 = bf16[32,128,512]{2,0,1:T(8,128)(2,1)S(1)} fusion(bf16[64,128,512]{2,1,0:T(8,128)(2,1)} %get-tuple-element.326, s32[32]{0:T(128)S(1)} %dynamic_slice.36), kind=kOutput, calls=%fused_computation.5.clone.1 | convolution fusion | flops 268437504 | bytes 12583040 | tf_op jit(solution)/shard_map/while/body/eval_jaxpr/gc,cjw->gjw/dot_general | solution.py:40
  264.0 6.3 %fusion.40 = bf16[32,128,512]{2,1,0:T(8,128)(2,1)S(1)} fusion(bf16[32,128,512]{2,0,1:T(8,128)(2,1)S(1)} %fusion.39, bf16[256,128,128]{2,1,0:T(8,128)(2,1)} %get-tuple-element.324, s32[]{:T(128)S(6)} %select_n.13), kind=kOutput, calls=%fused_computation.8.clone.1 | convolution fusion | flops 536870912 | bytes 9437188 | tf_op jit(solution)/shard_map/while/body/eval_jaxpr/gij,gjw->giw/dot_general | solution.py:43
  279.4 13.5 %fusion.39 = bf16[32,128,512]{2,0,1:T(8,128)(2,1)S(1)} fusion(bf16[64,128,512]{2,1,0:T(8,128)(2,1)} %get-tuple-element.326, s32[32]{0:T(128)S(1)} %dynamic_slice.36), kind=kOutput, calls=%fused_computation.5.clone.1 | convolution fusion | flops 268437504 | bytes 12583040 | tf_op jit(solution)/shard_map/while/body/eval_jaxpr/gc,cjw->gjw/dot_general | solution.py:40
  292.9 6.3 %fusion.40 = bf16[32,128,512]{2,1,0:T(8,128)(2,1)S(1)} fusion(bf16[32,128,512]{2,0,1:T(8,128)(2,1)S(1)} %fusion.39, bf16[256,128,128]{2,1,0:T(8,128)(2,1)} %get-tuple-element.324, s32[]{:T(128)S(6)} %select_n.13), kind=kOutput, calls=%fused_computation.8.clone.1 | convolution fusion | flops 536870912 | bytes 9437188 | tf_op jit(solution)/shard_map/while/body/eval_jaxpr/gij,gjw->giw/dot_general | solution.py:43
  308.3 13.5 %fusion.39 = bf16[32,128,512]{2,0,1:T(8,128)(2,1)S(1)} fusion(bf16[64,128,512]{2,1,0:T(8,128)(2,1)} %get-tuple-element.326, s32[32]{0:T(128)S(1)} %dynamic_slice.36), kind=kOutput, calls=%fused_computation.5.clone.1 | convolution fusion | flops 268437504 | bytes 12583040 | tf_op jit(solution)/shard_map/while/body/eval_jaxpr/gc,cjw->gjw/dot_general | solution.py:40
  321.8 6.3 %fusion.40 = bf16[32,128,512]{2,1,0:T(8,128)(2,1)S(1)} fusion(bf16[32,128,512]{2,0,1:T(8,128)(2,1)S(1)} %fusion.39, bf16[256,128,128]{2,1,0:T(8,128)(2,1)} %get-tuple-element.324, s32[]{:T(128)S(6)} %select_n.13), kind=kOutput, calls=%fused_computation.8.clone.1 | convolution fusion | flops 536870912 | bytes 9437188 | tf_op jit(solution)/shard_map/while/body/eval_jaxpr/gij,gjw->giw/dot_general | solution.py:43
  336.4 7.8 %copy.8 = bf16[32,128,512]{2,1,0:T(8,128)(2,1)S(1)} copy(f32[32,128,512]{2,0,1:T(8,128)} %get-tuple-element.188) | data formatting | bytes 12582912 | tf_op jit(solution)/shard_map/while | solution.py:51
  344.2 6.8 %fusion.22 = f32[4096,512]{0,1:T(8,128)} fusion(bf16[4096,512]{1,0:T(8,128)(2,1)S(1)} %bitcast.23, bf16[512,8704]{1,0:T(8,128)(2,1)} %all-gather.2.cloned.1.call-done), kind=kOutput, calls=%fused_computation.23 | convolution fusion | flops 2147483648 | bytes 13107200 | tf_op jit(solution)/shard_map/dot_general | solution.py:63
  351.0 52.0 %reduce-scatter.2.cloned.1.call-done = f32[4096,64]{0,1:T(8,128)} async-done(((f32[4096,512]{0,1:T(8,128)}), f32[4096,64]{0,1:T(8,128)}) %reduce-scatter.2.cloned.1.call-update) | async-done | bytes 1048592 | tf_op jit(solution)/shard_map/reduce_scatter | solution.py:66
  (95 shorter events, 71.9 us)
Async XLA Ops:
  6.5 79.0 %all-gather.2.cloned.1.call-start = ((), (), s32[]{:S(2)}) async-start(), calls=%async_computation.1 | async-start | bytes 9469952 | tf_op jit(solution)/shard_map/all_gather | solution.py:13
  8.5 394.5 %reduce-scatter.2.cloned.1.call-start = ((), (), s32[]{:S(2)}) async-start(), calls=%async_computation.2 | async-start | bytes 9437184 | tf_op jit(solution)/shard_map/reduce_scatter | solution.py:66
  105.9 20.0 %slice-start = ((s8[8388608]{0:T(1024)(128)(4,1)}), s8[4194304]{0:T(1024)(128)(4,1)S(1)}, s32[]{:S(2)}) async-start(s8[8388608]{0:T(1024)(128)(4,1)} %bitcast.21), calls=%async_computation.3 | async-start | bytes 8388608 | tf_op jit(solution)/shard_map/while
  105.9 19.9 %slice-start.1 = ((s8[8388608]{0:T(1024)(128)(4,1)}), s8[4194304]{0:T(1024)(128)(4,1)S(1)}, s32[]{:S(2)}) async-start(s8[8388608]{0:T(1024)(128)(4,1)} %bitcast.21), calls=%async_computation.4 | async-start | bytes 8388608 | tf_op jit(solution)/shard_map/while
  130.7 3.3 copy-start
  134.8 20.0 %slice-start = ((s8[8388608]{0:T(1024)(128)(4,1)}), s8[4194304]{0:T(1024)(128)(4,1)S(1)}, s32[]{:S(2)}) async-start(s8[8388608]{0:T(1024)(128)(4,1)} %bitcast.21), calls=%async_computation.3 | async-start | bytes 8388608 | tf_op jit(solution)/shard_map/while
  134.8 19.9 %slice-start.1 = ((s8[8388608]{0:T(1024)(128)(4,1)}), s8[4194304]{0:T(1024)(128)(4,1)S(1)}, s32[]{:S(2)}) async-start(s8[8388608]{0:T(1024)(128)(4,1)} %bitcast.21), calls=%async_computation.4 | async-start | bytes 8388608 | tf_op jit(solution)/shard_map/while
  159.6 3.3 copy-start
  163.7 20.0 %slice-start = ((s8[8388608]{0:T(1024)(128)(4,1)}), s8[4194304]{0:T(1024)(128)(4,1)S(1)}, s32[]{:S(2)}) async-start(s8[8388608]{0:T(1024)(128)(4,1)} %bitcast.21), calls=%async_computation.3 | async-start | bytes 8388608 | tf_op jit(solution)/shard_map/while
  163.7 19.9 %slice-start.1 = ((s8[8388608]{0:T(1024)(128)(4,1)}), s8[4194304]{0:T(1024)(128)(4,1)S(1)}, s32[]{:S(2)}) async-start(s8[8388608]{0:T(1024)(128)(4,1)} %bitcast.21), calls=%async_computation.4 | async-start | bytes 8388608 | tf_op jit(solution)/shard_map/while
  188.6 3.3 copy-start
  192.6 20.0 %slice-start = ((s8[8388608]{0:T(1024)(128)(4,1)}), s8[4194304]{0:T(1024)(128)(4,1)S(1)}, s32[]{:S(2)}) async-start(s8[8388608]{0:T(1024)(128)(4,1)} %bitcast.21), calls=%async_computation.3 | async-start | bytes 8388608 | tf_op jit(solution)/shard_map/while
  192.7 19.9 %slice-start.1 = ((s8[8388608]{0:T(1024)(128)(4,1)}), s8[4194304]{0:T(1024)(128)(4,1)S(1)}, s32[]{:S(2)}) async-start(s8[8388608]{0:T(1024)(128)(4,1)} %bitcast.21), calls=%async_computation.4 | async-start | bytes 8388608 | tf_op jit(solution)/shard_map/while
  217.5 3.3 copy-start
  221.5 20.0 %slice-start = ((s8[8388608]{0:T(1024)(128)(4,1)}), s8[4194304]{0:T(1024)(128)(4,1)S(1)}, s32[]{:S(2)}) async-start(s8[8388608]{0:T(1024)(128)(4,1)} %bitcast.21), calls=%async_computation.3 | async-start | bytes 8388608 | tf_op jit(solution)/shard_map/while
  221.6 19.9 %slice-start.1 = ((s8[8388608]{0:T(1024)(128)(4,1)}), s8[4194304]{0:T(1024)(128)(4,1)S(1)}, s32[]{:S(2)}) async-start(s8[8388608]{0:T(1024)(128)(4,1)} %bitcast.21), calls=%async_computation.4 | async-start | bytes 8388608 | tf_op jit(solution)/shard_map/while
  246.4 3.3 copy-start
  250.4 20.0 %slice-start = ((s8[8388608]{0:T(1024)(128)(4,1)}), s8[4194304]{0:T(1024)(128)(4,1)S(1)}, s32[]{:S(2)}) async-start(s8[8388608]{0:T(1024)(128)(4,1)} %bitcast.21), calls=%async_computation.3 | async-start | bytes 8388608 | tf_op jit(solution)/shard_map/while
  250.5 19.9 %slice-start.1 = ((s8[8388608]{0:T(1024)(128)(4,1)}), s8[4194304]{0:T(1024)(128)(4,1)S(1)}, s32[]{:S(2)}) async-start(s8[8388608]{0:T(1024)(128)(4,1)} %bitcast.21), calls=%async_computation.4 | async-start | bytes 8388608 | tf_op jit(solution)/shard_map/while
  275.3 3.3 copy-start
  279.3 20.0 %slice-start = ((s8[8388608]{0:T(1024)(128)(4,1)}), s8[4194304]{0:T(1024)(128)(4,1)S(1)}, s32[]{:S(2)}) async-start(s8[8388608]{0:T(1024)(128)(4,1)} %bitcast.21), calls=%async_computation.3 | async-start | bytes 8388608 | tf_op jit(solution)/shard_map/while
  279.4 19.9 %slice-start.1 = ((s8[8388608]{0:T(1024)(128)(4,1)}), s8[4194304]{0:T(1024)(128)(4,1)S(1)}, s32[]{:S(2)}) async-start(s8[8388608]{0:T(1024)(128)(4,1)} %bitcast.21), calls=%async_computation.4 | async-start | bytes 8388608 | tf_op jit(solution)/shard_map/while
  308.2 20.0 %slice-start = ((s8[8388608]{0:T(1024)(128)(4,1)}), s8[4194304]{0:T(1024)(128)(4,1)S(1)}, s32[]{:S(2)}) async-start(s8[8388608]{0:T(1024)(128)(4,1)} %bitcast.21), calls=%async_computation.3 | async-start | bytes 8388608 | tf_op jit(solution)/shard_map/while
  308.3 19.9 %slice-start.1 = ((s8[8388608]{0:T(1024)(128)(4,1)}), s8[4194304]{0:T(1024)(128)(4,1)S(1)}, s32[]{:S(2)}) async-start(s8[8388608]{0:T(1024)(128)(4,1)} %bitcast.21), calls=%async_computation.4 | async-start | bytes 8388608 | tf_op jit(solution)/shard_map/while
  (2 other events, 6.6 us)
Sparse Core Ops, SparseCore 0:
  9.5 76.0 all-gather.1
  351.1 51.8 reduce-scatter.1
where the time goes:
time: 413 us; the launch traced here: 412 us
  matrix products  205 us (50%)
  waiting for transfers between devices  128 us (31%)
  local copies, waits for them, and re-layouts  55.7 us (13%)
  between operations  13.4 us (3%)
  other arithmetic  9.22 us (2%)
    dot_general x8, matrix products, step(): jnp.einsum('gc,cjw->gjw', pick_cols, source, preferred_element_type=jnp.f...  108 us
    all_gather x1, waiting for transfers between devices, rows_first(): result = lax.all_gather(both, axis, axis=0, tiled=True)  76.2 us
    reduce_scatter x1, waiting for transfers between devices, body(): lax.psum_scatter(partial_value, 'col', scatter_dimension=1, tiled=True)  52 us
    dot_general x8, matrix products, step(): jnp.einsum('gij,gjw->giw', block, inputs, preferred_element_type=jnp.floa...  50.8 us
    dot_general x8, matrix products, step(): added = jnp.einsum('gt,giw->tiw', place_rows, prod)  39.2 us
    while x48, local copies, waits for them, and re-layouts  26.3 us
    transpose x2, local copies, waits for them, and re-layouts, rows_first(): jnp.moveaxis(b.reshape(-1, *t.shape[1:]), 0, dim)  19.5 us
  transfers between devices with their start and end apart: 2, of which 2 were waited for; matrix products, arithmetic and copies ran while one was open for 0% of the time, Pallas kernels for 0%

commit v1 on v0

v1 whole, which is shorter than its diff:
```python
import functools

import jax
import jax.numpy as jnp
from jax import lax
from jax.experimental import pallas as pl
from jax.experimental.pallas import tpu as pltpu
from jax.sharding import PartitionSpec as P

MESH = pl.DeviceIdType.MESH
SLOTS = 256
TROW = 32
PAIRS = 144
NODES_IN = 8192
F_OUT = 512
LANES = NODES_IN + F_OUT
HALF = LANES // 2
UNROLL = 8
BF16 = jnp.bfloat16
F32 = jnp.float32


def as_column(row):
    half = jnp.transpose(jnp.broadcast_to(row, (128, SLOTS)))
    return jnp.concatenate([half, half], axis=1)


def slot_order(rows, cols, count):
    slot = lax.broadcasted_iota(jnp.int32, (1, SLOTS), 1)
    live = slot < count
    rows = jnp.where(live, rows, 64)
    rows_c = as_column(rows)
    line = lax.broadcasted_iota(jnp.int32, (SLOTS, SLOTS), 0)
    lane = lax.broadcasted_iota(jnp.int32, (SLOTS, SLOTS), 1)
    rank = jnp.sum(jnp.where((rows_c == rows) & (line < lane), 1, 0), axis=0, keepdims=True)
    rank_c = as_column(rank)
    base = jnp.sum(jnp.where((rows_c < rows) & ((rank_c & 1) == 0), 1, 0), axis=0, keepdims=True)
    place = jnp.where(live, 2 * base + rank, 1 << 20)
    place_c = as_column(place)
    code = slot * 128 + cols * 2 + jnp.where(rank == 0, 0, 1)
    code_c = as_column(code)
    codes = []
    for block in range(3):
        spot = lax.broadcasted_iota(jnp.int32, (SLOTS, 128), 1) + block * 128
        here = place_c[:, :128] == spot
        found = jnp.sum(jnp.where(here, code_c[:, :128] + 1, 0), axis=0, keepdims=True)
        codes.append(jnp.where(found == 0, SLOTS * 128, found - 1))
    row_lane = lax.broadcasted_iota(jnp.int32, (SLOTS, 128), 1)
    last = jnp.max(
        jnp.where(rows_c[:, :128] == row_lane, place_c[:, :128] >> 1, -1), axis=0, keepdims=True
    )
    last = jnp.where(last < 0, PAIRS, last)
    return jnp.concatenate(codes, axis=1), last


def kernel(
    feat, weight, tiles, coords, count, out,
    f0, f1, f2, f3, turned, run, meta_v, meta_s, dsend, drecv, zsend, zrecv, own, total, osend,
    local_sem, p1_send, p1_recv, p2_send, p2_recv, d_send, d_recv, z_send, z_recv, o_send, o_recv,
):
    groups = (f0, f1, f2, f3)
    row, col = lax.axis_index("row"), lax.axis_index("col")
    y, x = row // 4, row % 4
    z, core = col // 2, col % 2

    def at_x(step):
        return (y * 4 + (x + step + 4) % 4, col)

    def at_y(step):
        return (((y + step + 4) % 4) * 4 + x, col)

    def at_col(dz, other):
        k = 1 - core if other else core
        return (row, ((z + dz) % 4) * 2 + k)

    def remote(src, dst, send, recv, device):
        return pltpu.make_async_remote_copy(
            src_ref=src, dst_ref=dst, send_sem=send, recv_sem=recv, device_id=device, device_id_type=MESH
        )

    loads = []
    for q in range(2):
        lines = pl.ds(q * 16, 16)
        into = pl.ds(q * 64, 16)
        loads.append((feat.at[lines], f0.at[into, pl.ds(0, NODES_IN)]))
        loads.append((weight.at[lines], f0.at[into, pl.ds(NODES_IN, F_OUT)]))
    loads.append((tiles, turned.at[pl.ds(0, SLOTS)]))
    loads = [pltpu.make_async_copy(a, b, local_sem.at[n]) for n, (a, b) in enumerate(loads)]
    for load in loads:
        load.start()

    barrier = pltpu.get_barrier_semaphore()
    peers = [at_x(1), at_x(-1), at_y(1), at_y(-1)]
    others = [(dz, o) for dz in range(4) for o in (0, 1) if (dz, o) != (0, 0)]
    peers += [at_col(dz, o) for dz, o in others]
    for peer in peers:
        pl.semaphore_signal(barrier, inc=1, device_id=peer, device_id_type=MESH)
    for load in loads[:4]:
        load.wait()
    pl.semaphore_wait(barrier, len(peers))

    def lanes(h):
        return pl.ds(h * HALF, HALF)

    def neighbour(q, d, phase):
        step = 1 if d == 0 else -1
        return at_x(step) if (q == 0) == (phase == 1) else at_y(step)

    phase1 = {}
    for step in range(3):
        for q in range(2):
            for d in range(2):
                h = (d, 1 - d, d)[step]
                src = (0, 0, 32 if d == 0 else 16)[step]
                dst = (32 if d == 0 else 16, 32 if d == 0 else 16, 48)[step]
                n = (q * 2 + d) * 3 + step
                phase1[q, d, step] = remote(
                    f0.at[pl.ds(64 * q + src, 16), lanes(h)],
                    f0.at[pl.ds(64 * q + dst, 16), lanes(h)],
                    p1_send.at[n], p1_recv.at[n], neighbour(q, d, 1),
                )
    for step in range(2):
        for q in range(2):
            for d in range(2):
                phase1[q, d, step].start()

    phase2 = {}
    for g in (1, 2, 3):
        for q in range(2):
            for b in range(4):
                d = int((b >= 2) == (g != 2))
                lines = pl.ds(64 * q + 16 * b, 16)
                src = f0 if g < 3 else f1
                n = ((g - 1) * 2 + q) * 4 + b
                phase2[g, q, b] = remote(
                    src.at[lines], groups[g].at[lines], p2_send.at[n], p2_recv.at[n], neighbour(q, d, 2)
                )

    codes, last = slot_order(coords[0:1, :], coords[1:2, :], count[0])
    meta_v[0:1, 0:384] = codes
    meta_v[1:2, 0:128] = last
    to_smem = pltpu.make_async_copy(meta_v, meta_s, local_sem.at[5])
    to_smem.start()

    run[PAIRS] = jnp.zeros((128, 128), F32)
    loads[4].wait()
    turned[SLOTS] = jnp.zeros((128, 128), BF16)

    def turn(lo, hi):
        def step(n, carry):
            for u in range(4):
                turned[lo + n * 4 + u] = jnp.transpose(turned[lo + n * 4 + u])
            return carry

        lax.fori_loop(0, (hi - lo) // 4, step, 0)

    turn(0, 64)
    for q in range(2):
        for d in range(2):
            phase1[q, d, 0].wait_recv()
            phase1[q, d, 2].start()
    for q in range(2):
        phase2[1, q, 0].start()
    turn(64, 160)
    for q in range(2):
        for d in range(2):
            phase1[q, d, 1].wait_recv()
    for q in range(2):
        phase2[1, q, 1].start()
        phase2[1, q, 2].start()
        phase2[2, q, 2].start()
    turn(160, 256)
    to_smem.wait()
    for q in range(2):
        for d in range(2):
            phase1[q, d, 2].wait_recv()
    for q in range(2):
        phase2[1, q, 3].start()
        phase2[2, q, 3].start()
        phase2[2, q, 0].start()
        phase2[2, q, 1].start()

    def apply(group):
        def step(n, acc):
            for u in range(UNROLL):
                p = n * UNROLL + u
                one = meta_s[0, 2 * p]
                two = meta_s[0, 2 * p + 1]
                lane1 = ((one >> 1) & 63) * 128
                lane2 = ((two >> 1) & 63) * 128
                left = jnp.concatenate([group[:, pl.ds(lane1, 128)], group[:, pl.ds(lane2, 128)]], axis=1)
                right = jnp.concatenate([turned[one >> 7], turned[two >> 7]], axis=0)
                prod = jnp.dot(left, right, preferred_element_type=F32)
                acc = acc * (one & 1).astype(F32) + prod
                run[p] = acc
            return acc

        lax.fori_loop(0, PAIRS // UNROLL, step, jnp.zeros((128, 128), F32))

    def to_pair(g):
        copy = remote(dsend.at[g], drecv.at[g], d_send.at[g], d_recv.at[g], at_col(0, 1))
        for dz in range(4):
            to = ((z + dz) % 4) * 2 + (1 - core)
            for u in range(4):
                dsend[g, dz, :, u * 128 : (u + 1) * 128] = run[meta_s[1, to * 4 + u]].astype(BF16)
        copy.start()
        return copy

    def to_planes(g, pair):
        pair.wait_recv()
        copies = []
        for dz in (1, 3, 2, 0):
            to = ((z + dz) % 4) * 2 + core
            for u in range(4):
                part = slice(u * 128, (u + 1) * 128)
                both = run[meta_s[1, to * 4 + u]] + drecv[g, dz, :, part].astype(F32)
                if dz:
                    zsend[g, dz - 1, :, part] = both.astype(BF16)
                else:
                    own[g, :, part] = both
            if dz:
                n = g * 3 + dz - 1
                copy = remote(zsend.at[g, dz - 1], zrecv.at[g, dz - 1], z_send.at[n], z_recv.at[n], at_col(dz, 0))
                copy.start()
                copies.append(copy)
        return copies

    def finish(g, copies):
        for copy in copies:
            copy.wait_recv()
        spread = own[g]
        for k in range(3):
            spread = spread + zrecv[g, k].astype(F32)
        part = lax.dot_general(
            groups[g][:, NODES_IN:LANES], spread.astype(BF16), (((0,), (0,)), ((), ())), preferred_element_type=F32
        )
        if g == 0:
            total[...] = part
        else:
            total[...] += part

    pairs, planes = {}, {}
    for g in range(4):
        if g == 1:
            for b in (0, 2, 1, 3):
                for q in range(2):
                    phase2[1, q, b].wait_recv()
                    phase2[3, q, b].start()
        elif g > 1:
            for q in range(2):
                for b in range(4):
                    phase2[g, q, b].wait_recv()
        apply(groups[g])
        pairs[g] = to_pair(g)
        if g:
            finish(g - 1, planes[g - 1])
        planes[g] = to_planes(g, pairs[g])
    finish(3, planes[3])

    outs = []
    for dz, o in [(1, 0), (1, 1), (3, 0), (3, 1), (2, 0), (2, 1), (0, 1)]:
        k = 1 - core if o else core
        to = ((z + dz) % 4) * 2 + k
        n = dz * 2 + o
        osend[n] = total[pl.ds(pl.multiple_of(to * 64, 64), 64), :].astype(BF16)
        copy = remote(
            osend.at[n], out.at[:, pl.ds(pl.multiple_of(col * 512, 512), 512)], o_send.at[n], o_recv.at[n], at_col(dz, o)
        )
        copy.start()
        outs.append(copy)
    out[:, pl.ds(pl.multiple_of(col * 512, 512), 512)] = total[pl.ds(pl.multiple_of(col * 64, 64), 64), :].astype(BF16)

    for copy in list(phase1.values()) + list(phase2.values()) + list(pairs.values()):
        copy.wait_send()
    for g in range(4):
        for copy in planes[g]:
            copy.wait_send()
    for copy in outs:
        copy.wait()


def body(features, weight_t, tiles, coords, counts):
    vmem = pl.BlockSpec(memory_space=pltpu.VMEM)
    anywhere = pl.BlockSpec(memory_space=pl.ANY)
    dma = pltpu.SemaphoreType.DMA
    out = pl.pallas_call(
        kernel,
        out_shape=jax.ShapeDtypeStruct((64, 4096), BF16),
        in_specs=[anywhere, anywhere, anywhere, vmem, pl.BlockSpec(memory_space=pltpu.SMEM)],
        out_specs=vmem,
        scratch_shapes=[
            *[pltpu.VMEM((128, LANES), BF16) for _ in range(4)],
            pltpu.VMEM((SLOTS + 1, 128, 128), BF16),
            pltpu.VMEM((PAIRS + 1, 128, 128), F32),
            pltpu.VMEM((8, 512), jnp.int32),
            pltpu.SMEM((8, 512), jnp.int32),
            pltpu.VMEM((4, 4, 128, 512), BF16),
            pltpu.VMEM((4, 4, 128, 512), BF16),
            pltpu.VMEM((4, 3, 128, 512), BF16),
            pltpu.VMEM((4, 3, 128, 512), BF16),
            pltpu.VMEM((4, 128, 512), F32),
            pltpu.VMEM((512, 512), F32),
            pltpu.VMEM((8, 64, 512), BF16),
            dma((6,)), dma((12,)), dma((12,)), dma((24,)), dma((24,)), dma((4,)), dma((4,)),
            dma((12,)), dma((12,)), dma((8,)), dma((8,)),
        ],
        compiler_params=pltpu.CompilerParams(
            collective_id=0, has_side_effects=True, vmem_limit_bytes=60 * 1024 * 1024
        ),
    )(features.T, weight_t.T, tiles, coords, counts)
    return out.T


def solution(mesh):
    placed = (
        P("col", "row"),
        P(None, "row"),
        P(("row", "col"), None, None),
        P(None, ("row", "col")),
        P(("row", "col")),
    )
    return jax.shard_map(
        body, mesh=mesh, in_specs=placed, out_specs=P("row", "col"), check_vma=False
    )
```

time: 413 us -> 82.5 us (0.20)
  matrix products: 205 us -> 0 us
  waiting for transfers between devices: 128 us -> 0 us
  Pallas kernels: 0 us -> 79.8 us
  local copies, waits for them, and re-layouts: 55.7 us -> 1.87 us
  between operations: 13.4 us -> 0.66 us
  other arithmetic: 9.22 us -> 0 us
    dot_general x25 -> x0, matrix products: 205 us -> none  [the longest x8 108 us: step(): jnp.einsum('gc,cjw->gjw', pick_cols, source, preferred_element_type=jnp.f...]
    pallas_call x0 -> x1, Pallas kernels: none -> 79.8 us  [body(): pl.pallas_call(kernel, out_shape=jax.ShapeDtypeStruct((64, 4096), BF16),...]
    all_gather x1 -> x0, waiting for transfers between devices: 76.2 us -> none  [rows_first(): result = lax.all_gather(both, axis, axis=0, tiled=True)]
    reduce_scatter x1 -> x0, waiting for transfers between devices: 52 us -> none  [body(): lax.psum_scatter(partial_value, 'col', scatter_dimension=1, tiled=True)]
    while x49 -> x0, local copies, waits for them, and re-layouts: 34.1 us -> none
    transpose x2 -> x0, local copies, waits for them, and re-layouts: 19.5 us -> none  [rows_first(): jnp.moveaxis(b.reshape(-1, *t.shape[1:]), 0, dim)]
    lt x8 -> x0, other arithmetic: 5.2 us -> none  [step(): live = start + offsets < count]
  transfers between devices with their start and end apart: 2 -> 0, of which waited for: 2 -> 0; matrix products, arithmetic and copies ran while one was open for 0% -> 0% of each run, Pallas kernels for 0% -> 0%
where the time goes in v1:
time: 82.5 us; the launch traced here: 82.4 us
  Pallas kernels  79.8 us (97%)
  local copies, waits for them, and re-layouts  1.87 us (2%)
    pallas_call x1, Pallas kernels, body(): pl.pallas_call(kernel, out_shape=jax.ShapeDtypeStruct((64, 4096), BF16),...  79.8 us
    unnamed x1, local copies, waits for them, and re-layouts  1.87 us

profile of v1, /device:TPU:1, one launch (start us, length us, event | category | flops | bytes accessed | tf_op | source)
XLA Modules:
  0.0 82.4 jit_solution(17654443324319870734)
XLA Ops:
  0.7 79.8 %shard_map.55 = bf16[64,4096]{1,0:T(8,128)(2,1)} custom-call(bf16[32,8192]{1,0:T(8,128)(2,1)} %bitcast.4, bf16[32,512]{1,0:T(8,128)(2,1)} %bitcast.5, bf16[256,128,128]{2,1,0:T(8,128)(2,1)} %tiles.1, s32[2,256]{1,0:T(2,128)} %coords.1, s32[1]{0:T(128)S(6)} %copy.7.count), custom_call_target="tpu_custom_call" | custom-call | tf_op jit(solution)/shard_map/pallas_call | solution.py:286
  80.5 1.9 %copy.8 = bf16[4096,64]{0,1:T(8,128)(2,1)} copy(bf16[4096,64]{0,1:T(8,128)(2,1)} %bitcast.3) | data formatting | bytes 1048576

commit v2 on v1

v2 whole, which is shorter than its diff:
```python
import functools

import jax
import jax.numpy as jnp
from jax import lax
from jax.experimental import pallas as pl
from jax.experimental.pallas import tpu as pltpu
from jax.sharding import PartitionSpec as P

MESH = pl.DeviceIdType.MESH
SLOTS = 256
TROW = 32
PAIRS = 144
NODES_IN = 8192
O_PART = 128
LANES = NODES_IN + O_PART
HALF = 4096
UNROLL = 48
BF16 = jnp.bfloat16
F32 = jnp.float32


def phase(name):
    return jax.named_scope(name)


def as_column(row):
    half = jnp.transpose(jnp.broadcast_to(row, (128, SLOTS)))
    return jnp.concatenate([half, half], axis=1)


def slot_order(rows, cols, count):
    slot = lax.broadcasted_iota(jnp.int32, (1, SLOTS), 1)
    live = slot < count
    rows = jnp.where(live, rows, 64)
    rows_c = as_column(rows)
    line = lax.broadcasted_iota(jnp.int32, (SLOTS, SLOTS), 0)
    lane = lax.broadcasted_iota(jnp.int32, (SLOTS, SLOTS), 1)
    rank = jnp.sum(jnp.where((rows_c == rows) & (line < lane), 1, 0), axis=0, keepdims=True)
    rank_c = as_column(rank)
    base = jnp.sum(jnp.where((rows_c < rows) & ((rank_c & 1) == 0), 1, 0), axis=0, keepdims=True)
    place = jnp.where(live, 2 * base + rank, 1 << 20)
    place_c = as_column(place)
    code = slot * 128 + cols * 2 + jnp.where(rank == 0, 0, 1)
    code_c = as_column(code)
    codes = []
    for block in range(3):
        spot = lax.broadcasted_iota(jnp.int32, (SLOTS, 128), 1) + block * 128
        here = place_c[:, :128] == spot
        found = jnp.sum(jnp.where(here, code_c[:, :128] + 1, 0), axis=0, keepdims=True)
        codes.append(jnp.where(found == 0, SLOTS * 128, found - 1))
    row_lane = lax.broadcasted_iota(jnp.int32, (SLOTS, 128), 1)
    last = jnp.max(
        jnp.where(rows_c[:, :128] == row_lane, place_c[:, :128] >> 1, -1), axis=0, keepdims=True
    )
    last = jnp.where(last < 0, PAIRS, last)
    return jnp.concatenate(codes, axis=1), last


def kernel(
    feat, weight, tiles, coords, counts, out,
    f0, f1, f2, f3, f4, turned, run, places, count, meta_v, meta_s,
    dsend, drecv, zsend, zrecv, own, wparts, total, osend,
    local_sem, p1_send, p1_recv, p2_send, p2_recv, w_send, w_recv,
    d_send, d_recv, z_send, z_recv, o_send, o_recv,
):
    groups = (f0, f1, f2, f3, f4)
    depth = [group.shape[0] for group in groups]
    row, col = lax.axis_index("row"), lax.axis_index("col")
    y, x = row // 4, row % 4
    z, core = col // 2, col % 2

    def at_x(step):
        return (y * 4 + (x + step + 4) % 4, col)

    def at_y(step):
        return (((y + step + 4) % 4) * 4 + x, col)

    def at_col(dz, other):
        k = 1 - core if other else core
        return (row, ((z + dz) % 4) * 2 + k)

    def remote(src, dst, send, recv, device):
        return pltpu.make_async_remote_copy(
            src_ref=src, dst_ref=dst, send_sem=send, recv_sem=recv, device_id=device, device_id_type=MESH
        )

    barrier = pltpu.get_barrier_semaphore()
    peers = [at_col(dz, o) for dz in (2, 1, 3, 0) for o in (0, 1) if (dz, o) != (0, 0)]
    peers = peers[:6] + [at_x(1), at_x(-1), at_y(1), at_y(-1)] + peers[6:]
    for peer in peers:
        pl.semaphore_signal(barrier, inc=1, device_id=peer, device_id_type=MESH)

    loads = []
    for q in range(2):
        lines = pl.ds(q * 16, 16)
        into = pl.ds(q * 64, 16)
        loads.append((feat.at[lines], f0.at[into, pl.ds(0, NODES_IN)]))
        part = pl.ds(pl.multiple_of(z * O_PART, O_PART), O_PART)
        loads.append((weight.at[lines, part], f0.at[into, pl.ds(NODES_IN, O_PART)]))
    loads += [(coords, places), (counts, count)]
    loads.append((tiles, turned.at[pl.ds(0, SLOTS)]))
    loads = [pltpu.make_async_copy(a, b, local_sem.at[n]) for n, (a, b) in enumerate(loads)]
    for load in loads:
        load.start()
    with phase("loads"):
        for load in loads[:4]:
            load.wait()
    with phase("barrier"):
        pl.semaphore_wait(barrier, len(peers))

    def lanes(h):
        return pl.ds(h * HALF, HALF if h == 0 else LANES - HALF)

    def neighbour(q, d, phase):
        step = 1 if d == 0 else -1
        return at_x(step) if (q == 0) == (phase == 1) else at_y(step)

    both = [(q, d) for q in range(2) for d in range(2)]
    phase1 = {}
    for step in range(3):
        for q, d in both:
            h = (d, 1 - d, d)[step]
            src = (0, 0, 32 if d == 0 else 16)[step]
            dst = (32 if d == 0 else 16, 32 if d == 0 else 16, 48)[step]
            n = (q * 2 + d) * 3 + step
            phase1[q, d, step] = remote(
                f0.at[pl.ds(64 * q + src, 16), lanes(h)],
                f0.at[pl.ds(64 * q + dst, 16), lanes(h)],
                p1_send.at[n], p1_recv.at[n], neighbour(q, d, 1),
            )

    phase2 = {}
    for q, d in both:
        for k in range(6):
            if k < 4:
                src, line = f0, 64 * q + 16 * k
                dst, to = (f1, f2)[k // 2], 64 * q + 32 * d + 16 * (k % 2)
            else:
                src, line = (f1, f2)[d], 64 * q + 32 * d + 16 * (k - 4)
                dst, to = (f3, f4)[k - 4], 32 * q + 16 * d
            n = (q * 2 + d) * 6 + k
            phase2[q, d, k] = remote(
                src.at[pl.ds(line, 16)], dst.at[pl.ds(to, 16)], p2_send.at[n], p2_recv.at[n], neighbour(q, d, 2)
            )

    for step in range(2):
        for q, d in both:
            phase1[q, d, step].start()
    for q, d in both:
        phase2[q, d, 0].start()

    loads[4].wait()
    loads[5].wait()
    with phase("order"):
        codes, last = slot_order(places[0:1, :], places[1:2, :], count[0])
        meta_v[0:1, 0:384] = codes
        meta_v[1:2, 0:128] = last
    to_smem = pltpu.make_async_copy(meta_v, meta_s, local_sem.at[7])
    to_smem.start()

    run[PAIRS] = jnp.zeros((128, 128), F32)
    loads[6].wait()
    turned[SLOTS] = jnp.zeros((128, 128), BF16)

    def turn(lo, hi):
        def step(n, carry):
            for u in range(4):
                turned[lo + n * 4 + u] = jnp.transpose(turned[lo + n * 4 + u])
            return carry

        lax.fori_loop(0, (hi - lo) // 4, step, 0)

    with phase("turn0"):
        turn(0, 64)
    with phase("p1_0"):
        for q, d in both:
            phase1[q, d, 0].wait_recv()
            phase1[q, d, 2].start()
    with phase("turn1"):
        turn(64, 160)
    with phase("p1_1"):
        for q, d in both:
            phase1[q, d, 1].wait_recv()
        for k in (1, 2):
            for q, d in both:
                phase2[q, d, k].start()
    with phase("turn2"):
        turn(160, 256)
    to_smem.wait()
    with phase("p1_2"):
        for q, d in both:
            phase1[q, d, 2].wait_recv()
        for q, d in both:
            phase2[q, d, 3].start()

    def share_weight(g):
        lines = pl.ds(0, depth[g])
        for dz in (1, 3, 2):
            n = g * 3 + dz - 1
            copy = remote(
                groups[g].at[:, pl.ds(NODES_IN, O_PART)], wparts.at[g, dz - 1, lines],
                w_send.at[n], w_recv.at[n], at_col(dz, 0),
            )
            copy.start()
            shared.append(copy)

    shared = []

    def apply(g):
        group, lines = groups[g], depth[g]

        def step(n, acc):
            for u in range(UNROLL):
                p = n * UNROLL + u
                one = meta_s[0, 2 * p]
                two = meta_s[0, 2 * p + 1]
                lane1 = ((one >> 1) & 63) * 128
                lane2 = ((two >> 1) & 63) * 128
                left = jnp.concatenate([group[:, pl.ds(lane1, 128)], group[:, pl.ds(lane2, 128)]], axis=1)
                right = jnp.concatenate([turned[one >> 7], turned[two >> 7]], axis=0)
                prod = jnp.dot(left, right, preferred_element_type=F32)
                acc = acc * (one & 1).astype(F32) + prod
                run[p, 0:lines] = acc
            return acc

        lax.fori_loop(0, PAIRS // UNROLL, step, jnp.zeros((lines, 128), F32))

    def to_pair(g, part, parts):
        lines, n = depth[g], g + part
        share = 4 // parts
        here = pl.ds(part * share * 128, share * 128)
        copy = remote(
            dsend.at[g, :, pl.ds(0, lines), here], drecv.at[g, :, pl.ds(0, lines), here],
            d_send.at[n], d_recv.at[n], at_col(0, 1),
        )
        for dz in range(4):
            to = ((z + dz) % 4) * 2 + (1 - core)
            for u in range(part * share, (part + 1) * share):
                dsend[g, dz, 0:lines, u * 128 : (u + 1) * 128] = run[meta_s[1, to * 4 + u], 0:lines].astype(BF16)
        copy.start()
        return copy

    def to_planes(g, part, parts, pair):
        lines = depth[g]
        share = 4 // parts
        here = pl.ds(part * share * 128, share * 128)
        with phase("pair_wait"):
            pair.wait_recv()
        copies = []
        for dz in (2, 1, 3, 0):
            to = ((z + dz) % 4) * 2 + core
            for u in range(part * share, (part + 1) * share):
                at = slice(u * 128, (u + 1) * 128)
                summed = run[meta_s[1, to * 4 + u], 0:lines] + drecv[g, dz, 0:lines, at].astype(F32)
                if dz:
                    zsend[g, dz - 1, 0:lines, at] = summed.astype(BF16)
                else:
                    own[g, 0:lines, at] = summed
            if dz:
                n = (g + part) * 3 + dz - 1
                copy = remote(
                    zsend.at[g, dz - 1, pl.ds(0, lines), here], zrecv.at[g, dz - 1, pl.ds(0, lines), here],
                    z_send.at[n], z_recv.at[n], at_col(dz, 0),
                )
                copy.start()
                copies.append(copy)
        return copies

    def finish(g, part, parts, copies):
        lines = depth[g]
        width = 512 // parts
        at = slice(part * width, (part + 1) * width)
        with phase("plane_wait"):
            for copy in copies:
                copy.wait_recv()
            if part == 0:
                for copy in shared[3 * g : 3 * g + 3]:
                    copy.wait_recv()
        spread = own[g, 0:lines, at]
        for k in range(3):
            spread = spread + zrecv[g, k, 0:lines, at].astype(F32)
        spread = spread.astype(BF16)
        for dz in range(4):
            if dz:
                piece = wparts[g, dz - 1, 0:lines]
            else:
                piece = groups[g][:, NODES_IN:LANES]
            product = lax.dot_general(piece, spread, (((0,), (0,)), ((), ())), preferred_element_type=F32)
            to = pl.ds(pl.multiple_of(((z - dz + 4) % 4) * O_PART, O_PART), O_PART)
            if g == 0:
                total[to, at] = product
            else:
                total[to, at] += product

    pairs, planes = [], []

    def partial_sums(g):
        share_weight(g)
        parts = 2 if g == 4 else 1
        with phase(f"apply{g}"):
            apply(g)
        for part in range(parts):
            with phase(f"to_pair{g}"):
                pairs.append(to_pair(g, part, parts))
        for part in range(parts):
            with phase(f"to_planes{g}"):
                planes.append(to_planes(g, part, parts, pairs[g + part]))

    def done(g):
        with phase(f"finish{g}"):
            finish(g, 0, 1, planes[g])

    partial_sums(0)
    with phase("p2_1"):
        for k in (0, 1):
            for q, d in both:
                phase2[q, d, k].wait_recv()
                if d == 0:
                    phase2[q, d, k + 4].start()
    partial_sums(1)
    with phase("p2_2"):
        for k in (2, 3):
            for q, d in both[::-1]:
                phase2[q, d, k].wait_recv()
                if d == 1:
                    phase2[q, d, k + 2].start()
    partial_sums(2)
    done(0)
    with phase("p2_3"):
        for q, d in both:
            phase2[q, d, 4].wait_recv()
    partial_sums(3)
    done(1)
    with phase("p2_4"):
        for q, d in both:
            phase2[q, d, 5].wait_recv()
    partial_sums(4)
    done(2)
    done(3)

    outs = []
    for part in range(2):
        with phase(f"finish{4 + part}"):
            finish(4, part, 2, planes[4 + part])
        at = slice(part * 256, part * 256 + 256)
        here = pl.ds(pl.multiple_of(col * 512 + part * 256, 256), 256)
        for dz, o in [(2, 0), (2, 1), (1, 0), (1, 1), (3, 0), (3, 1), (0, 1)]:
            k = 1 - core if o else core
            to = ((z + dz) % 4) * 2 + k
            n = part * 8 + dz * 2 + o
            osend[n] = total[pl.ds(pl.multiple_of(to * 64, 64), 64), at].astype(BF16)
            copy = remote(osend.at[n], out.at[:, here], o_send.at[n], o_recv.at[n], at_col(dz, o))
            copy.start()
            outs.append(copy)
        out[:, here] = total[pl.ds(pl.multiple_of(col * 64, 64), 64), at].astype(BF16)

    with phase("drain"):
        for copy in list(phase1.values()) + list(phase2.values()) + pairs + sum(planes, []) + shared:
            copy.wait_send()
    with phase("out_wait"):
        for copy in outs:
            copy.wait()


def body(features, weight_t, tiles, coords, counts):
    anywhere = pl.BlockSpec(memory_space=pl.ANY)
    dma = pltpu.SemaphoreType.DMA
    out = pl.pallas_call(
        kernel,
        out_shape=jax.ShapeDtypeStruct((64, 4096), BF16),
        in_specs=[anywhere] * 5,
        out_specs=pl.BlockSpec(memory_space=pltpu.VMEM),
        scratch_shapes=[
            *[pltpu.VMEM((lines, LANES), BF16) for lines in (128, 128, 128, 64, 64)],
            pltpu.VMEM((SLOTS + 1, 128, 128), BF16),
            pltpu.VMEM((PAIRS + 1, 128, 128), F32),
            pltpu.VMEM((2, SLOTS), jnp.int32),
            pltpu.SMEM((1,), jnp.int32),
            pltpu.VMEM((8, 512), jnp.int32),
            pltpu.SMEM((8, 512), jnp.int32),
            pltpu.VMEM((5, 4, 128, 512), BF16),
            pltpu.VMEM((5, 4, 128, 512), BF16),
            pltpu.VMEM((5, 3, 128, 512), BF16),
            pltpu.VMEM((5, 3, 128, 512), BF16),
            pltpu.VMEM((5, 128, 512), F32),
            pltpu.VMEM((5, 3, 128, O_PART), BF16),
            pltpu.VMEM((512, 512), F32),
            pltpu.VMEM((16, 64, 256), BF16),
            dma((8,)), dma((12,)), dma((12,)), dma((24,)), dma((24,)), dma((15,)), dma((15,)),
            dma((6,)), dma((6,)), dma((18,)), dma((18,)), dma((16,)), dma((16,)),
        ],
        compiler_params=pltpu.CompilerParams(
            collective_id=0, has_side_effects=True, vmem_limit_bytes=60 * 1024 * 1024
        ),
    )(features.T, weight_t.T, tiles, coords, counts)
    return out.T


def solution(mesh):
    placed = (
        P("col", "row"),
        P(None, "row"),
        P(("row", "col"), None, None),
        P(None, ("row", "col")),
        P(("row", "col")),
    )
    return jax.shard_map(
        body, mesh=mesh, in_specs=placed, out_specs=P("row", "col"), check_vma=False
    )
```

time: 82.5 us -> 73.1 us (0.89)
  Pallas kernels: 79.8 us -> 70.4 us
    pallas_call x1, Pallas kernels: 79.8 us -> 70.4 us  [body(): pl.pallas_call(kernel, out_shape=jax.ShapeDtypeStruct((64, 4096), BF16),...]
where the time goes in v2:
time: 73.1 us; the launch traced here: 73 us
  Pallas kernels  70.4 us (96%)
  local copies, waits for them, and re-layouts  1.87 us (3%)
    pallas_call x1, Pallas kernels, body(): pl.pallas_call(kernel, out_shape=jax.ShapeDtypeStruct((64, 4096), BF16),...  70.4 us
    unnamed x1, local copies, waits for them, and re-layouts  1.87 us

profile of v2, /device:TPU:1, one launch (start us, length us, event | category | flops | bytes accessed | tf_op | source)
XLA Modules:
  0.0 73.0 jit_solution(12636490415182995868)
XLA Ops:
  0.7 70.4 %shard_map.55 = bf16[64,4096]{1,0:T(8,128)(2,1)} custom-call(bf16[32,8192]{1,0:T(8,128)(2,1)} %bitcast.4, bf16[32,512]{1,0:T(8,128)(2,1)} %bitcast.5, bf16[256,128,128]{2,1,0:T(8,128)(2,1)} %tiles.1, s32[2,256]{1,0:T(2,128)} %coords.1, s32[1]{0:T(128)S(6)} %copy.7.counts), custom_call_target="tpu_custom_call" | custom-call | tf_op jit(solution)/shard_map/pallas_call | solution.py:369
  71.1 1.9 %copy.8 = bf16[4096,64]{0,1:T(8,128)(2,1)} copy(bf16[4096,64]{0,1:T(8,128)(2,1)} %bitcast.3) | data formatting | bytes 1048576
